TPU v7x, 32 devices: a whole 2x2x4 slice. The times are simulated.
32 devices in a mesh: ty: 4 (over y, x), tx: 8 (over z, core).
Axes of the slice: x: 2, y: 2, z: 4, core: 2. Of those that a mesh axis runs over, the one named last changes fastest.
Arguments:
- object_slices: float32 [2, 2, 1024, 2048], P(None, None, 'ty', 'tx'), may hold values from -5 to 5
- probe: float32 [2, 256, 256], replicated, may hold values from -5 to 5
- position_count: int32 [4, 8], P('ty', 'tx'), may hold values from 1 to 5, as said below
- offsets: int32 [4, 8, 5, 2], P('ty', 'tx'), may hold values from 0 to 128
- intensities: float32 [4, 8, 5, 256, 256], P('ty', 'tx'), may hold values from 0 to 2
Outputs:
- object_new: float32 [2, 2, 1024, 2048], P(None, None, 'ty', 'tx')
- probe_new: float32 [2, 256, 256], replicated
Inputs may be any that keep to these rules, and one draw needn't show every extreme that they name: `position_count`: each tile has 1 to 5 positions; some tile has exactly 5.
All inputs are finite; a program needn't handle non-finite values.
Results may differ from a plain program's by a relative error of at most 0.0003.
Values sent between devices are 32-bit elements; how exact they have to be, the bound alone decides.
No kernel may reach another device: no remote copies, remote signals or barrier semaphores. Data moves between devices by JAX's collectives and lax.ppermute only.
A program may use at most 128 MiB of HBM per device.

v0:
```python
import math
import jax
import jax.numpy as jnp
from jax import lax
from jax.sharding import PartitionSpec as P

PROBE = 256
CORE = 256
MARGIN = 64
ITERS = 2
chirp_rate = 0.5
object_rate = 0.5
probe_rate = 2.0


def extended_2(block, sides, width):
    for axis, dim in sides:
        count = lax.axis_size(axis)
        forward = [(i, i + 1) for i in range(count - 1)]
        forward.append((count - 1, 0))
        backward = [(target, source) for source, target in forward]
        low = lax.ppermute(
            lax.slice_in_dim(block, block.shape[dim] - width, None, axis=dim), axis, forward
        )
        high = lax.ppermute(lax.slice_in_dim(block, 0, width, axis=dim), axis, backward)
        block = jnp.concatenate([low, block, high], axis=dim)
    return block


def matmul(left, right):
    return jnp.dot(left, right, precision=lax.Precision.HIGHEST, preferred_element_type=jnp.float32)


def complex_product(left_real, left_imag, right_real, right_imag):
    out_real = matmul(left_real, right_real) - matmul(left_imag, right_imag)
    out_imag = matmul(left_real, right_imag) + matmul(left_imag, right_real)
    return (out_real, out_imag)


def dft_tables(size):
    index = lax.iota(jnp.int32, size)
    product = index[:, None] * index[None, :] % size
    angles = product.astype(jnp.float32) * (2.0 * math.pi / size)
    factor = 1.0 / math.sqrt(size)
    four_real = jnp.cos(angles) * factor
    four_imag = -jnp.sin(angles) * factor
    centred = ((index + size // 2) % size - size // 2).astype(jnp.float32)
    phases = centred * centred * (chirp_rate * math.pi / size)
    kernel_real = jnp.cos(phases)
    kernel_imag = -jnp.sin(phases)
    scaled_real = four_real * kernel_real[None, :] + four_imag * kernel_imag[None, :]
    scaled_imag = four_real * kernel_imag[None, :] - four_imag * kernel_real[None, :]
    prop_real, prop_imag = complex_product(scaled_real, scaled_imag, four_real, four_imag)
    return (four_real, four_imag, prop_real, prop_imag)


def forward_pair(mat_real, mat_imag, field_real, field_imag):
    mid_real, mid_imag = complex_product(mat_real, mat_imag, field_real, field_imag)
    return complex_product(mid_real, mid_imag, mat_real.T, mat_imag.T)


def adjoint_pair(mat_real, mat_imag, field_real, field_imag):
    mid_real, mid_imag = complex_product(mat_real.T, -mat_imag.T, field_real, field_imag)
    return complex_product(mid_real, mid_imag, mat_real, -mat_imag)


def position_grad(probe_now, window, measured, tables):
    four_real, four_imag, prop_real, prop_imag = tables
    probe_real, probe_imag = (probe_now[0], probe_now[1])
    one_real, one_imag, two_real, two_imag = (window[0], window[1], window[2], window[3])
    wave_real = probe_real * one_real - probe_imag * one_imag
    wave_imag = probe_real * one_imag + probe_imag * one_real
    moved_real, moved_imag = forward_pair(prop_real, prop_imag, wave_real, wave_imag)
    exit_real = moved_real * two_real - moved_imag * two_imag
    exit_imag = moved_real * two_imag + moved_imag * two_real
    far_real, far_imag = forward_pair(four_real, four_imag, exit_real, exit_imag)
    misfit = far_real * far_real + far_imag * far_imag - measured
    back_real, back_imag = adjoint_pair(four_real, four_imag, misfit * far_real, misfit * far_imag)
    grad_two_real = moved_real * back_real + moved_imag * back_imag
    grad_two_imag = moved_real * back_imag - moved_imag * back_real
    gmove_real = two_real * back_real + two_imag * back_imag
    gmove_imag = two_real * back_imag - two_imag * back_real
    gwave_real, gwave_imag = adjoint_pair(prop_real, prop_imag, gmove_real, gmove_imag)
    grad_one_real = probe_real * gwave_real + probe_imag * gwave_imag
    grad_one_imag = probe_real * gwave_imag - probe_imag * gwave_real
    gprobe_real = one_real * gwave_real + one_imag * gwave_imag
    gprobe_imag = one_real * gwave_imag - one_imag * gwave_real
    object_part = jnp.stack([grad_one_real, grad_one_imag, grad_two_real, grad_two_imag])
    return (object_part, jnp.stack([gprobe_real, gprobe_imag]))


def fold_axis(padded, width, dim):
    extent = padded.shape[dim] - 2 * width
    middle = lax.slice_in_dim(padded, width, width + extent, axis=dim)
    before = lax.slice_in_dim(padded, 0, width, axis=dim)
    after = lax.slice_in_dim(padded, width + extent, extent + 2 * width, axis=dim)
    spec_before = [(0, 0)] * padded.ndim
    spec_before[dim] = (2 * MARGIN - width, extent - 2 * MARGIN)
    spec_after = [(0, 0)] * padded.ndim
    spec_after[dim] = (CORE, extent - CORE - width)
    return middle + jnp.pad(before, spec_before) + jnp.pad(after, spec_after)


def fold_sums(padded, width):
    return fold_axis(fold_axis(padded, width, 1), width, 2)


def body(object_slices, probe, position_count, offsets, intensities):
    tables = dft_tables(PROBE)
    extent = CORE + 2 * MARGIN
    zero = jnp.int32(0)
    count = position_count[0, 0]
    core = object_slices.reshape(4, CORE, CORE)
    extended = extended_2(core, (("ty", 1), ("tx", 2)), MARGIN)
    probe_now = probe
    devices = lax.axis_size("ty") * lax.axis_size("tx")
    for step in range(ITERS):

        def visit(slot, carry):
            local, local_probe = carry
            top = offsets[0, 0, slot, 0]
            left = offsets[0, 0, slot, 1]
            window = lax.dynamic_slice(extended, (zero, top, left), (4, PROBE, PROBE))
            object_part, probe_part = position_grad(
                probe_now, window, intensities[0, 0, slot], tables
            )
            current = lax.dynamic_slice(local, (zero, top, left), (4, PROBE, PROBE))
            local = lax.dynamic_update_slice(local, current + object_part, (zero, top, left))
            return (local, local_probe + probe_part)

        start = (
            jnp.zeros((4, extent, extent), jnp.float32),
            jnp.zeros((2, PROBE, PROBE), jnp.float32),
        )
        grads, probe_grad = lax.fori_loop(zero, count, visit, start)
        peak = jnp.max(probe_now[0] * probe_now[0] + probe_now[1] * probe_now[1]) + 1e-06
        padded = extended_2(grads, (("ty", 1), ("tx", 2)), MARGIN)
        total = fold_sums(padded, MARGIN)[:, MARGIN : MARGIN + CORE, MARGIN : MARGIN + CORE]
        core = core - object_rate / peak * total
        if step + 1 < ITERS:
            extended = extended_2(core, (("ty", 1), ("tx", 2)), MARGIN)
        summed = lax.psum(probe_grad, ("ty", "tx"))
        probe_now = probe_now - probe_rate / devices * summed
    return (core.reshape(2, 2, CORE, CORE), probe_now)


def solution(mesh):
    placed = (
        P(None, None, "ty", "tx"),
        P(),
        P("ty", "tx"),
        P("ty", "tx", None, None),
        P("ty", "tx", None, None, None),
    )
    return jax.shard_map(
        body,
        mesh=mesh,
        in_specs=placed,
        out_specs=(P(None, None, "ty", "tx"), P()),
        check_vma=False,
    )
```

profile of v0, /device:TPU:0, one launch (start us, length us, event | category | flops | bytes accessed | tf_op | source)
XLA Modules:
  0.0 1035.9 jit_solution(13837448059332774943)
XLA Ops:
  17.1 9.8 collective-permute-done
  26.9 10.6 %collective-permute-done.1 = f32[4,64,256]{1,2,0:T(8,128)S(1)} collective-permute-done((f32[4,64,256]{1,2,0:T(8,128)}, f32[4,64,256]{1,2,0:T(8,128)S(1)}, u32[]{:S(2)}, u32[]{:S(2)}) %collective-permute-start.1) | collective-permute-done | bytes 262176 | tf_op jit(solution)/shard_map/ppermute | solution.py:25
  38.0 3.5 collective-permute-start.3
  44.5 4.6 collective-permute-done.2
  54.6 203.5 %while.32 = (s32[]{:T(128)}, f32[4,384,384]{2,1,0:T(8,128)}, f32[2,256,256]{2,1,0:T(8,128)}, s32[]{:T(128)}, s32[1,1,5,2]{2,3,1,0:T(2,128)S(1)}, /*index=5*/f32[...) while((s32[]{:T(128)}, f32[4,384,384]{2,1,0:T(8,128)}, ...), condition=%wide.region_2.3_spmd.clone.clone, body=%wide.region_1.2_spmd.clone.clone.sunk | while | flops 6464077824 | bytes 48234916 | solution.py:135
  125.1 11.5 %dynamic_update_slice.16 = f32[4,384,384]{2,1,0:T(8,128)} dynamic-update-slice(f32[4,384,384]{2,1,0:T(8,128)} %get-tuple-element.1014, f32[4,256,256]{2,1,0:T(8,128)S(1)} %maximum_add_fusion.8, s32[]{:T(128)} %constant.70.clone.1..sunk, s32[]{:T(128)S(6)} %select_n.366, s32[]{:T(128)S(6)} %select_n.367) | dynamic-update-slice | bytes 2097156 | tf_op jit(solution)/shard_map/while/body/dynamic_update_slice | solution.py:128
  183.1 11.3 %dynamic_update_slice.16 = f32[4,384,384]{2,1,0:T(8,128)} dynamic-update-slice(f32[4,384,384]{2,1,0:T(8,128)} %get-tuple-element.1014, f32[4,256,256]{2,1,0:T(8,128)S(1)} %maximum_add_fusion.8, s32[]{:T(128)} %constant.70.clone.1..sunk, s32[]{:T(128)S(6)} %select_n.366, s32[]{:T(128)S(6)} %select_n.367) | dynamic-update-slice | bytes 2097156 | tf_op jit(solution)/shard_map/while/body/dynamic_update_slice | solution.py:128
  240.9 11.5 %dynamic_update_slice.16 = f32[4,384,384]{2,1,0:T(8,128)} dynamic-update-slice(f32[4,384,384]{2,1,0:T(8,128)} %get-tuple-element.1014, f32[4,256,256]{2,1,0:T(8,128)S(1)} %maximum_add_fusion.8, s32[]{:T(128)} %constant.70.clone.1..sunk, s32[]{:T(128)S(6)} %select_n.366, s32[]{:T(128)S(6)} %select_n.367) | dynamic-update-slice | bytes 2097156 | tf_op jit(solution)/shard_map/while/body/dynamic_update_slice | solution.py:128
  259.3 117.1 %collective-permute-start.5 = (f32[4,64,384]{2,1,0:T(8,128)S(1)}, f32[4,64,384]{2,1,0:T(8,128)S(1)}, u32[]{:S(2)}, u32[]{:S(2)}) collective-permute-start(f32[4,64,384]{2,1,0:T(8,128)S(1)} %get-tuple-element.749), channel_id=1, source_target_pairs={{8,0},{16,8},{24,16},{0,24},{9,1},{17,9},{25,17},{1,25},{10,2},{18... | collective-permute-start | bytes 1179656 | tf_op jit(solution)/shard_map/ppermute | solution.py:25
  379.5 4.3 collective-permute-done.4
  388.7 4.3 collective-permute-start.6
  394.3 7.8 collective-permute-done.6
  413.8 8.9 collective-permute-start.8
  422.7 13.3 %collective-permute-done.8 = f32[4,64,256]{1,2,0:T(8,128)S(1)} collective-permute-done((f32[4,64,256]{1,2,0:T(8,128)}, f32[4,64,256]{1,2,0:T(8,128)S(1)}, u32[]{:S(2)}, u32[]{:S(2)}) %collective-permute-start.8) | collective-permute-done | bytes 262176 | tf_op jit(solution)/shard_map/ppermute | solution.py:22
  436.0 11.2 %collective-permute-done.9 = f32[4,64,256]{1,2,0:T(8,128)} collective-permute-done((f32[4,64,256]{1,2,0:T(8,128)}, f32[4,64,256]{1,2,0:T(8,128)}, u32[]{:S(2)}, u32[]{:S(2)}) %collective-permute-start.9) | collective-permute-done | bytes 262176 | tf_op jit(solution)/shard_map/ppermute | solution.py:25
  449.4 3.5 collective-permute-start.11
  452.9 100.7 %all-reduce.11.cloned.1.call-done = f32[2,256,256]{2,1,0:T(8,128)} async-done(((f32[2,256,256]{2,1,0:T(8,128)}), f32[2,256,256]{2,1,0:T(8,128)}) %all-reduce.11.cloned.1.call-update) | async-done | bytes 524304 | tf_op jit(solution)/shard_map/psum | solution.py:142
  560.5 204.1 %while.33 = (s32[]{:T(128)}, f32[4,384,384]{2,1,0:T(8,128)}, f32[2,256,256]{2,1,0:T(8,128)}, s32[]{:T(128)}, s32[1,1,5,2]{2,3,1,0:T(2,128)S(1)}, /*index=5*/f32[...) while((s32[]{:T(128)}, f32[4,384,384]{2,1,0:T(8,128)}, ...), condition=%wide.region_6.7_spmd.clone.clone, body=%wide.region_5.6_spmd.clone.clone.sunk | while | flops 6464077824 | bytes 48234916 | solution.py:135
  631.4 11.5 %dynamic_update_slice.17 = f32[4,384,384]{2,1,0:T(8,128)} dynamic-update-slice(f32[4,384,384]{2,1,0:T(8,128)} %get-tuple-element.1071, f32[4,256,256]{2,1,0:T(8,128)S(1)} %maximum_add_fusion.10, s32[]{:T(128)} %constant.70.clone.1..sunk.1, s32[]{:T(128)S(6)} %select_n.385, s32[]{:T(128)S(6)} %select_n.386) | dynamic-update-slice | bytes 2097156 | tf_op jit(solution)/shard_map/while/body/dynamic_update_slice | solution.py:128
  690.0 11.3 %dynamic_update_slice.17 = f32[4,384,384]{2,1,0:T(8,128)} dynamic-update-slice(f32[4,384,384]{2,1,0:T(8,128)} %get-tuple-element.1071, f32[4,256,256]{2,1,0:T(8,128)S(1)} %maximum_add_fusion.10, s32[]{:T(128)} %constant.70.clone.1..sunk.1, s32[]{:T(128)S(6)} %select_n.385, s32[]{:T(128)S(6)} %select_n.386) | dynamic-update-slice | bytes 2097156 | tf_op jit(solution)/shard_map/while/body/dynamic_update_slice | solution.py:128
  748.5 11.5 %dynamic_update_slice.17 = f32[4,384,384]{2,1,0:T(8,128)} dynamic-update-slice(f32[4,384,384]{2,1,0:T(8,128)} %get-tuple-element.1071, f32[4,256,256]{2,1,0:T(8,128)S(1)} %maximum_add_fusion.10, s32[]{:T(128)} %constant.70.clone.1..sunk.1, s32[]{:T(128)S(6)} %select_n.385, s32[]{:T(128)S(6)} %select_n.386) | dynamic-update-slice | bytes 2097156 | tf_op jit(solution)/shard_map/while/body/dynamic_update_slice | solution.py:128
  765.8 119.2 %collective-permute-start.13 = (f32[4,64,384]{2,1,0:T(8,128)S(1)}, f32[4,64,384]{2,1,0:T(8,128)S(1)}, u32[]{:S(2)}, u32[]{:S(2)}) collective-permute-start(f32[4,64,384]{2,1,0:T(8,128)S(1)} %get-tuple-element.747), channel_id=1, source_target_pairs={{8,0},{16,8},{24,16},{0,24},{9,1},{17,9},{25,17},{1,25},{10,2},{18... | collective-permute-start | bytes 1179656 | tf_op jit(solution)/shard_map/ppermute | solution.py:25
  888.1 6.8 collective-permute-done.12
  902.9 116.5 %all-reduce.13.cloned.1.call-done = f32[2,256,256]{2,1,0:T(8,128)} async-done(((f32[2,256,256]{2,1,0:T(8,128)}), f32[2,256,256]{2,1,0:T(8,128)}) %all-reduce.13.cloned.1.call-update) | async-done | bytes 524304 | tf_op jit(solution)/shard_map/psum | solution.py:142
  (355 shorter events, 324.2 us)
Async XLA Ops:
  7.2 546.4 %all-reduce.11.cloned.1.call-start = ((), (), s32[]{:S(2)}) async-start(), calls=%async_computation | async-start | bytes 1048576 | tf_op jit(solution)/shard_map/psum | solution.py:142
  8.8 40.3 %copy-start.3 = (f32[2,2,256,256]{2,3,1,0:T(8,128)}, f32[2,2,256,256]{2,3,1,0:T(8,128)S(1)}, u32[]{:S(2)}) copy-start(f32[2,2,256,256]{2,3,1,0:T(8,128)S(1)} %copy.21) | copy-start | bytes 3145732
  10.0 16.9 %collective-permute-start = (f32[4,64,256]{1,2,0:T(8,128)}, f32[4,64,256]{1,2,0:T(8,128)S(1)}, u32[]{:S(2)}, u32[]{:S(2)}) collective-permute-start(f32[4,64,256]{1,2,0:T(8,128)} %get-tuple-element.756), channel_id=1, source_target_pairs={{0,8},{8,16},{16,24},{24,0},{1,9},{9,17},{17,25},{25,1},{2,10},{10... | collective-permute-start | bytes 786440 | tf_op jit(solution)/shard_map/ppermute | solution.py:22
  13.0 24.6 %collective-permute-start.1 = (f32[4,64,256]{1,2,0:T(8,128)}, f32[4,64,256]{1,2,0:T(8,128)S(1)}, u32[]{:S(2)}, u32[]{:S(2)}) collective-permute-start(f32[4,64,256]{1,2,0:T(8,128)} %get-tuple-element.757), channel_id=1, source_target_pairs={{8,0},{16,8},{24,16},{0,24},{9,1},{17,9},{25,17},{1,25},{10,2},{18... | collective-permute-start | bytes 786440 | tf_op jit(solution)/shard_map/ppermute | solution.py:25
  37.9 11.2 %collective-permute-start.2 = (f32[4,384,64]{1,2,0:T(8,128)S(1)}, f32[4,384,64]{1,2,0:T(8,128)S(1)}, u32[]{:S(2)}, u32[]{:S(2)}) collective-permute-start(f32[4,384,64]{1,2,0:T(8,128)S(1)} %get-tuple-element.752), channel_id=1, source_target_pairs={{0,1},{1,2},{2,3},{3,4},{4,5},{5,6},{6,7},{7,0},{8,9},{9,10},{10,1... | collective-permute-start | bytes 1179656 | tf_op jit(solution)/shard_map/ppermute | solution.py:22
  38.0 11.1 %collective-permute-start.3 = (f32[4,384,64]{1,2,0:T(8,128)S(1)}, f32[4,384,64]{1,2,0:T(8,128)S(1)}, u32[]{:S(2)}, u32[]{:S(2)}) collective-permute-start(f32[4,384,64]{1,2,0:T(8,128)S(1)} %get-tuple-element.753), channel_id=1, source_target_pairs={{1,0},{2,1},{3,2},{4,3},{5,4},{6,5},{7,6},{0,7},{9,8},{10,9},{11,1... | collective-permute-start | bytes 1179656 | tf_op jit(solution)/shard_map/ppermute | solution.py:25
  123.1 13.5 %copy-start.10 = (f32[2,256,256]{2,1,0:T(8,128)}, f32[2,256,256]{2,1,0:T(8,128)S(1)}, u32[]{:S(2)}) copy-start(f32[2,256,256]{2,1,0:T(8,128)S(1)} %maximum_add_fusion.9) | copy-start | bytes 1572868 | tf_op jit(solution)/shard_map/while
  238.9 13.5 %copy-start.10 = (f32[2,256,256]{2,1,0:T(8,128)}, f32[2,256,256]{2,1,0:T(8,128)S(1)}, u32[]{:S(2)}) copy-start(f32[2,256,256]{2,1,0:T(8,128)S(1)} %maximum_add_fusion.9) | copy-start | bytes 1572868 | tf_op jit(solution)/shard_map/while
  259.3 124.5 %collective-permute-start.4 = (f32[4,64,384]{2,1,0:T(8,128)S(1)}, f32[4,64,384]{2,1,0:T(8,128)}, u32[]{:S(2)}, u32[]{:S(2)}) collective-permute-start(f32[4,64,384]{2,1,0:T(8,128)S(1)} %get-tuple-element.748), channel_id=1, source_target_pairs={{0,8},{8,16},{16,24},{24,0},{1,9},{9,17},{17,25},{25,1},{2,10},{10... | collective-permute-start | bytes 1179656 | tf_op jit(solution)/shard_map/ppermute | solution.py:22
  259.3 126.6 %collective-permute-start.5 = (f32[4,64,384]{2,1,0:T(8,128)S(1)}, f32[4,64,384]{2,1,0:T(8,128)S(1)}, u32[]{:S(2)}, u32[]{:S(2)}) collective-permute-start(f32[4,64,384]{2,1,0:T(8,128)S(1)} %get-tuple-element.749), channel_id=1, source_target_pairs={{8,0},{16,8},{24,16},{0,24},{9,1},{17,9},{25,17},{1,25},{10,2},{18... | collective-permute-start | bytes 1179656 | tf_op jit(solution)/shard_map/ppermute | solution.py:25
  388.7 13.5 %collective-permute-start.6 = (f32[4,512,64]{1,2,0:T(8,128)}, f32[4,512,64]{1,2,0:T(8,128)}, u32[]{:S(2)}, u32[]{:S(2)}) collective-permute-start(f32[4,512,64]{1,2,0:T(8,128)} %get-tuple-element.740), channel_id=1, source_target_pairs={{0,1},{1,2},{2,3},{3,4},{4,5},{5,6},{6,7},{7,0},{8,9},{9,10},{10,1... | collective-permute-start | bytes 1572872 | tf_op jit(solution)/shard_map/ppermute | solution.py:22
  393.0 11.9 %collective-permute-start.7 = (f32[4,512,64]{1,2,0:T(8,128)}, f32[4,512,64]{1,2,0:T(8,128)}, u32[]{:S(2)}, u32[]{:S(2)}) collective-permute-start(f32[4,512,64]{1,2,0:T(8,128)} %get-tuple-element.741), channel_id=1, source_target_pairs={{1,0},{2,1},{3,2},{4,3},{5,4},{6,5},{7,6},{0,7},{9,8},{10,9},{11,1... | collective-permute-start | bytes 1572872 | tf_op jit(solution)/shard_map/ppermute | solution.py:25
  394.3 13.6 %copy-start.2 = (f32[4,384,384]{1,2,0:T(8,128)S(1)}, f32[4,384,384]{1,2,0:T(8,128)}, u32[]{:S(2)}) copy-start(f32[4,384,384]{1,2,0:T(8,128)} %copy.25) | copy-start | bytes 7077892
  412.5 142.2 %copy-start.5 = (f32[4,256,256]{1,2,0:T(8,128)}, f32[4,256,256]{1,2,0:T(8,128)S(1)}, u32[]{:S(2)}) copy-start(f32[4,256,256]{1,2,0:T(8,128)S(1)} %fusion.249) | copy-start | bytes 3145732
  413.8 22.2 %collective-permute-start.8 = (f32[4,64,256]{1,2,0:T(8,128)}, f32[4,64,256]{1,2,0:T(8,128)S(1)}, u32[]{:S(2)}, u32[]{:S(2)}) collective-permute-start(f32[4,64,256]{1,2,0:T(8,128)} %get-tuple-element.754), channel_id=1, source_target_pairs={{0,8},{8,16},{16,24},{24,0},{1,9},{9,17},{17,25},{25,1},{2,10},{10... | collective-permute-start | bytes 786440 | tf_op jit(solution)/shard_map/ppermute | solution.py:22
  422.6 24.5 %collective-permute-start.9 = (f32[4,64,256]{1,2,0:T(8,128)}, f32[4,64,256]{1,2,0:T(8,128)}, u32[]{:S(2)}, u32[]{:S(2)}) collective-permute-start(f32[4,64,256]{1,2,0:T(8,128)} %get-tuple-element.755), channel_id=1, source_target_pairs={{8,0},{16,8},{24,16},{0,24},{9,1},{17,9},{25,17},{1,25},{10,2},{18... | collective-permute-start | bytes 786440 | tf_op jit(solution)/shard_map/ppermute | solution.py:25
  422.7 596.7 %all-reduce.13.cloned.1.call-start = ((), (), s32[]{:S(2)}) async-start(), calls=%async_computation.1 | async-start | bytes 1048576 | tf_op jit(solution)/shard_map/psum | solution.py:142
  436.0 17.0 %copy-start.11 = (f32[4,64,256]{1,2,0:T(8,128)}, f32[4,64,256]{1,2,0:T(8,128)S(1)}, u32[]{:S(2)}) copy-start(f32[4,64,256]{1,2,0:T(8,128)S(1)} %collective-permute-done.8) | copy-start | bytes 786436
  449.4 105.3 %collective-permute-start.10 = (f32[4,384,64]{1,2,0:T(8,128)}, f32[4,384,64]{1,2,0:T(8,128)S(1)}, u32[]{:S(2)}, u32[]{:S(2)}) collective-permute-start(f32[4,384,64]{1,2,0:T(8,128)} %get-tuple-element.750), channel_id=1, source_target_pairs={{0,1},{1,2},{2,3},{3,4},{4,5},{5,6},{6,7},{7,0},{8,9},{9,10},{10,1... | collective-permute-start | bytes 1179656 | tf_op jit(solution)/shard_map/ppermute | solution.py:22
  449.4 105.3 %collective-permute-start.11 = (f32[4,384,64]{1,2,0:T(8,128)}, f32[4,384,64]{1,2,0:T(8,128)}, u32[]{:S(2)}, u32[]{:S(2)}) collective-permute-start(f32[4,384,64]{1,2,0:T(8,128)} %get-tuple-element.751), channel_id=1, source_target_pairs={{1,0},{2,1},{3,2},{4,3},{5,4},{6,5},{7,6},{0,7},{9,8},{10,9},{11,1... | collective-permute-start | bytes 1179656 | tf_op jit(solution)/shard_map/ppermute | solution.py:25
  765.8 129.1 %collective-permute-start.12 = (f32[4,64,384]{2,1,0:T(8,128)S(1)}, f32[4,64,384]{2,1,0:T(8,128)S(1)}, u32[]{:S(2)}, u32[]{:S(2)}) collective-permute-start(f32[4,64,384]{2,1,0:T(8,128)S(1)} %get-tuple-element.746), channel_id=1, source_target_pairs={{0,8},{8,16},{16,24},{24,0},{1,9},{9,17},{17,25},{25,1},{2,10},{10... | collective-permute-start | bytes 1179656 | tf_op jit(solution)/shard_map/ppermute | solution.py:22
  765.8 129.3 %collective-permute-start.13 = (f32[4,64,384]{2,1,0:T(8,128)S(1)}, f32[4,64,384]{2,1,0:T(8,128)S(1)}, u32[]{:S(2)}, u32[]{:S(2)}) collective-permute-start(f32[4,64,384]{2,1,0:T(8,128)S(1)} %get-tuple-element.747), channel_id=1, source_target_pairs={{8,0},{16,8},{24,16},{0,24},{9,1},{17,9},{25,17},{1,25},{10,2},{18... | collective-permute-start | bytes 1179656 | tf_op jit(solution)/shard_map/ppermute | solution.py:25
  898.0 123.3 %collective-permute-start.14 = (f32[4,512,64]{1,2,0:T(8,128)}, f32[4,512,64]{1,2,0:T(8,128)S(1)}, u32[]{:S(2)}, u32[]{:S(2)}) collective-permute-start(f32[4,512,64]{1,2,0:T(8,128)} %get-tuple-element.738), channel_id=1, source_target_pairs={{0,1},{1,2},{2,3},{3,4},{4,5},{5,6},{6,7},{7,0},{8,9},{9,10},{10,1... | collective-permute-start | bytes 1572872 | tf_op jit(solution)/shard_map/ppermute | solution.py:22
  898.1 123.1 %collective-permute-start.15 = (f32[4,512,64]{1,2,0:T(8,128)}, f32[4,512,64]{1,2,0:T(8,128)S(1)}, u32[]{:S(2)}, u32[]{:S(2)}) collective-permute-start(f32[4,512,64]{1,2,0:T(8,128)} %get-tuple-element.739), channel_id=1, source_target_pairs={{1,0},{2,1},{3,2},{4,3},{5,4},{6,5},{7,6},{0,7},{9,8},{10,9},{11,1... | collective-permute-start | bytes 1572872 | tf_op jit(solution)/shard_map/ppermute | solution.py:25
  (16 other events, 65.5 us)
Sparse Core Ops, SparseCore 0:
  422.8 130.7 all-reduce.10
  888.2 131.0 all-reduce.12
where the time goes:
time: 1050 us; the launch traced here: 1040 us
  waiting for transfers between devices  289 us (28%)
  starting transfers between devices  264 us (25%)
  matrix products  211 us (20%)
  local copies, waits for them, and re-layouts  128 us (12%)
  loops' own time  85.2 us (8%)
  other arithmetic  42.3 us (4%)
  between operations  15.9 us (2%)
    ppermute x8, starting transfers between devices, extended_2(): lax.ppermute(lax.slice_in_dim(block, 0, width, axis=dim), axis, backward)  248 us
    psum x2, waiting for transfers between devices, body(): summed = lax.psum(probe_grad, ('ty', 'tx'))  217 us
    dot_general x196, matrix products, matmul(): jnp.dot(left, right, precision=lax.Precision.HIGHEST, preferred_element_t...  211 us
    another operation x2, loops' own time, body(): grads, probe_grad = lax.fori_loop(zero, count, visit, start)  85.2 us
    dynamic_update_slice x6, local copies, waits for them, and re-layouts, visit(): lax.dynamic_update_slice(local, current + object_part, (zero, top, left))  68.5 us
    ppermute x8, waiting for transfers between devices, extended_2(): lax.ppermute(lax.slice_in_dim(block, block.shape[dim] - width, None, axis...  46.6 us
    ppermute x8, waiting for transfers between devices, extended_2(): lax.ppermute(lax.slice_in_dim(block, 0, width, axis=dim), axis, backward)  25.5 us
  transfers between devices with their start and end apart: 18, of which 12 were waited for; matrix products, arithmetic and copies ran while one was open for 2% of the time, Pallas kernels for 0%

commit v1 on v0

--- a/solution.py
+++ b/solution.py
@@ -139,7 +139,8 @@
         core = core - object_rate / peak * total
         if step + 1 < ITERS:
             extended = extended_2(core, (("ty", 1), ("tx", 2)), MARGIN)
-        summed = lax.psum(probe_grad, ("ty", "tx"))
+        row_out = lax.all_gather(probe_grad, ("ty", "tx"))
+        summed = jnp.sum(row_out, axis=0)
         probe_now = probe_now - probe_rate / devices * summed
     return (core.reshape(2, 2, CORE, CORE), probe_now)
 

time: 1050 us -> 987 us (0.940)
  waiting for transfers between devices: 289 us -> 196 us
  starting transfers between devices: 264 us -> 284 us
    psum x2 -> x0, waiting for transfers between devices: 217 us -> none  [body(): summed = lax.psum(probe_grad, ('ty', 'tx'))]
    all_gather x0 -> x2, waiting for transfers between devices: none -> 86.8 us  [body(): row_out = lax.all_gather(probe_grad, ('ty', 'tx'))]
    ppermute x8, starting transfers between devices: 16.4 us -> 41.8 us  [extended_2(): lax.ppermute(lax.slice_in_dim(block, block.shape[dim] - width, None, axis...]
    ppermute x8, waiting for transfers between devices: 25.5 us -> 50.1 us  [extended_2(): lax.ppermute(lax.slice_in_dim(block, 0, width, axis=dim), axis, backward)]
    reduce_sum x0 -> x2, other arithmetic: none -> 13.8 us  [body(): summed = jnp.sum(row_out, axis=0)]
    ppermute x8, waiting for transfers between devices: 46.6 us -> 59 us  [extended_2(): lax.ppermute(lax.slice_in_dim(block, block.shape[dim] - width, None, axis...]
  transfers between devices with their start and end apart: 18 -> 18, of which waited for: 12 -> 16; matrix products, arithmetic and copies ran while one was open for 2% -> 4% of each run, Pallas kernels for 0% -> 0%
where the time goes in v1:
time: 987 us; the launch traced here: 975 us
  starting transfers between devices  284 us (29%)
  matrix products  211 us (21%)
  waiting for transfers between devices  196 us (20%)
  local copies, waits for them, and re-layouts  128 us (13%)
  loops' own time  88.1 us (9%)
  other arithmetic  52.7 us (5%)
  between operations  15.8 us (2%)
    ppermute x8, starting transfers between devices, extended_2(): lax.ppermute(lax.slice_in_dim(block, 0, width, axis=dim), axis, backward)  242 us
    dot_general x196, matrix products, matmul(): jnp.dot(left, right, precision=lax.Precision.HIGHEST, preferred_element_t...  211 us
    another operation x2, loops' own time, body(): grads, probe_grad = lax.fori_loop(zero, count, visit, start)  88.1 us
    all_gather x2, waiting for transfers between devices, body(): row_out = lax.all_gather(probe_grad, ('ty', 'tx'))  86.8 us
    dynamic_update_slice x6, local copies, waits for them, and re-layouts, visit(): lax.dynamic_update_slice(local, current + object_part, (zero, top, left))  68.7 us
    ppermute x8, waiting for transfers between devices, extended_2(): lax.ppermute(lax.slice_in_dim(block, block.shape[dim] - width, None, axis...  59 us
    ppermute x8, waiting for transfers between devices, extended_2(): lax.ppermute(lax.slice_in_dim(block, 0, width, axis=dim), axis, backward)  50.1 us
    ppermute x8, starting transfers between devices, extended_2(): lax.ppermute(lax.slice_in_dim(block, block.shape[dim] - width, None, axis...  41.8 us
  transfers between devices with their start and end apart: 18, of which 16 were waited for; matrix products, arithmetic and copies ran while one was open for 4% of the time, Pallas kernels for 0%

profile of v1, /device:TPU:0, one launch (start us, length us, event | category | flops | bytes accessed | tf_op | source)
XLA Modules:
  0.0 975.1 jit_solution(4038876512988222311)
XLA Ops:
  17.2 9.8 %collective-permute-done = f32[4,64,256]{1,2,0:T(8,128)S(1)} collective-permute-done((f32[4,64,256]{1,2,0:T(8,128)}, f32[4,64,256]{1,2,0:T(8,128)S(1)}, u32[]{:S(2)}, u32[]{:S(2)}) %collective-permute-start) | collective-permute-done | bytes 262176 | tf_op jit(solution)/shard_map/ppermute | solution.py:22
  27.0 10.6 %collective-permute-done.1 = f32[4,64,256]{1,2,0:T(8,128)S(1)} collective-permute-done((f32[4,64,256]{1,2,0:T(8,128)}, f32[4,64,256]{1,2,0:T(8,128)S(1)}, u32[]{:S(2)}, u32[]{:S(2)}) %collective-permute-start.1) | collective-permute-done | bytes 262176 | tf_op jit(solution)/shard_map/ppermute | solution.py:25
  54.6 205.7 %while.32 = (s32[]{:T(128)}, f32[4,384,384]{2,1,0:T(8,128)}, f32[2,256,256]{2,1,0:T(8,128)}, s32[]{:T(128)}, s32[1,1,5,2]{2,3,1,0:T(2,128)S(1)}, /*index=5*/f32[...) while((s32[]{:T(128)}, f32[4,384,384]{2,1,0:T(8,128)}, ...), condition=%wide.region_2.3_spmd.clone.clone, body=%wide.region_1.2_spmd.clone.clone.sunk | while | flops 6464077824 | bytes 48234916 | solution.py:135
  125.5 11.5 %dynamic_update_slice.16 = f32[4,384,384]{2,1,0:T(8,128)} dynamic-update-slice(f32[4,384,384]{2,1,0:T(8,128)} %get-tuple-element.1014, f32[4,256,256]{2,1,0:T(8,128)S(1)} %maximum_add_fusion.8, s32[]{:T(128)} %constant.71.clone.1..sunk, s32[]{:T(128)S(6)} %select_n.366, s32[]{:T(128)S(6)} %select_n.367) | dynamic-update-slice | bytes 2097156 | tf_op jit(solution)/shard_map/while/body/dynamic_update_slice | solution.py:128
  184.0 11.3 %dynamic_update_slice.16 = f32[4,384,384]{2,1,0:T(8,128)} dynamic-update-slice(f32[4,384,384]{2,1,0:T(8,128)} %get-tuple-element.1014, f32[4,256,256]{2,1,0:T(8,128)S(1)} %maximum_add_fusion.8, s32[]{:T(128)} %constant.71.clone.1..sunk, s32[]{:T(128)S(6)} %select_n.366, s32[]{:T(128)S(6)} %select_n.367) | dynamic-update-slice | bytes 2097156 | tf_op jit(solution)/shard_map/while/body/dynamic_update_slice | solution.py:128
  242.4 11.5 %dynamic_update_slice.16 = f32[4,384,384]{2,1,0:T(8,128)} dynamic-update-slice(f32[4,384,384]{2,1,0:T(8,128)} %get-tuple-element.1014, f32[4,256,256]{2,1,0:T(8,128)S(1)} %maximum_add_fusion.8, s32[]{:T(128)} %constant.71.clone.1..sunk, s32[]{:T(128)S(6)} %select_n.366, s32[]{:T(128)S(6)} %select_n.367) | dynamic-update-slice | bytes 2097156 | tf_op jit(solution)/shard_map/while/body/dynamic_update_slice | solution.py:128
  261.6 118.0 %collective-permute-start.5 = (f32[4,64,384]{2,1,0:T(8,128)S(1)}, f32[4,64,384]{2,1,0:T(8,128)S(1)}, u32[]{:S(2)}, u32[]{:S(2)}) collective-permute-start(f32[4,64,384]{2,1,0:T(8,128)S(1)} %get-tuple-element.749), channel_id=1, source_target_pairs={{8,0},{16,8},{24,16},{0,24},{9,1},{17,9},{25,17},{1,25},{10,2},{18... | collective-permute-start | bytes 1179656 | tf_op jit(solution)/shard_map/ppermute | solution.py:25
  401.2 13.0 %collective-permute-done.6 = f32[4,512,64]{1,2,0:T(8,128)} collective-permute-done((f32[4,512,64]{1,2,0:T(8,128)}, f32[4,512,64]{1,2,0:T(8,128)}, u32[]{:S(2)}, u32[]{:S(2)}) %collective-permute-start.6) | collective-permute-done | bytes 524320 | tf_op jit(solution)/shard_map/ppermute | solution.py:22
  422.2 13.4 %collective-permute-start.8 = (f32[4,64,256]{1,2,0:T(8,128)S(1)}, f32[4,64,256]{1,2,0:T(8,128)S(1)}, u32[]{:S(2)}, u32[]{:S(2)}) collective-permute-start(f32[4,64,256]{1,2,0:T(8,128)S(1)} %get-tuple-element.754), channel_id=1, source_target_pairs={{0,8},{8,16},{16,24},{24,0},{1,9},{9,17},{17,25},{25,1},{2,10},{10... | collective-permute-start | bytes 786440 | tf_op jit(solution)/shard_map/ppermute | solution.py:22
  435.6 7.3 collective-permute-done.8
  442.9 18.6 %collective-permute-done.9 = f32[4,64,256]{1,2,0:T(8,128)S(1)} collective-permute-done((f32[4,64,256]{1,2,0:T(8,128)S(1)}, f32[4,64,256]{1,2,0:T(8,128)S(1)}, u32[]{:S(2)}, u32[]{:S(2)}) %collective-permute-start.9) | collective-permute-done | bytes 262176 | tf_op jit(solution)/shard_map/ppermute | solution.py:25
  463.6 16.5 %collective-permute-start.10 = (f32[4,384,64]{1,2,0:T(8,128)}, f32[4,384,64]{1,2,0:T(8,128)S(1)}, u32[]{:S(2)}, u32[]{:S(2)}) collective-permute-start(f32[4,384,64]{1,2,0:T(8,128)} %get-tuple-element.750), channel_id=1, source_target_pairs={{0,1},{1,2},{2,3},{3,4},{4,5},{5,6},{6,7},{7,0},{8,9},{9,10},{10,1... | collective-permute-start | bytes 1179656 | tf_op jit(solution)/shard_map/ppermute | solution.py:22
  481.7 14.0 %collective-permute-done.11 = f32[4,384,64]{1,2,0:T(8,128)} collective-permute-done((f32[4,384,64]{1,2,0:T(8,128)}, f32[4,384,64]{1,2,0:T(8,128)}, u32[]{:S(2)}, u32[]{:S(2)}) %collective-permute-start.11) | collective-permute-done | bytes 393248 | tf_op jit(solution)/shard_map/ppermute | solution.py:25
  498.8 9.6 all-gather.5.cloned.1.call-done
  508.4 6.9 reduce_sum.18
  517.8 204.7 %while.33 = (s32[]{:T(128)}, f32[4,384,384]{2,1,0:T(8,128)}, f32[2,256,256]{2,1,0:T(8,128)}, s32[]{:T(128)}, s32[1,1,5,2]{2,3,1,0:T(2,128)S(1)}, /*index=5*/f32[...) while((s32[]{:T(128)}, f32[4,384,384]{2,1,0:T(8,128)}, ...), condition=%wide.region_6.7_spmd.clone.clone, body=%wide.region_5.6_spmd.clone.clone.sunk | while | flops 6464077824 | bytes 48234916 | solution.py:135
  588.7 11.5 %dynamic_update_slice.17 = f32[4,384,384]{2,1,0:T(8,128)} dynamic-update-slice(f32[4,384,384]{2,1,0:T(8,128)} %get-tuple-element.1071, f32[4,256,256]{2,1,0:T(8,128)S(1)} %maximum_add_fusion.10, s32[]{:T(128)} %constant.71.clone.1..sunk.1, s32[]{:T(128)S(6)} %select_n.385, s32[]{:T(128)S(6)} %select_n.386) | dynamic-update-slice | bytes 2097156 | tf_op jit(solution)/shard_map/while/body/dynamic_update_slice | solution.py:128
  647.2 11.3 %dynamic_update_slice.17 = f32[4,384,384]{2,1,0:T(8,128)} dynamic-update-slice(f32[4,384,384]{2,1,0:T(8,128)} %get-tuple-element.1071, f32[4,256,256]{2,1,0:T(8,128)S(1)} %maximum_add_fusion.10, s32[]{:T(128)} %constant.71.clone.1..sunk.1, s32[]{:T(128)S(6)} %select_n.385, s32[]{:T(128)S(6)} %select_n.386) | dynamic-update-slice | bytes 2097156 | tf_op jit(solution)/shard_map/while/body/dynamic_update_slice | solution.py:128
  705.6 11.5 %dynamic_update_slice.17 = f32[4,384,384]{2,1,0:T(8,128)} dynamic-update-slice(f32[4,384,384]{2,1,0:T(8,128)} %get-tuple-element.1071, f32[4,256,256]{2,1,0:T(8,128)S(1)} %maximum_add_fusion.10, s32[]{:T(128)} %constant.71.clone.1..sunk.1, s32[]{:T(128)S(6)} %select_n.385, s32[]{:T(128)S(6)} %select_n.386) | dynamic-update-slice | bytes 2097156 | tf_op jit(solution)/shard_map/while/body/dynamic_update_slice | solution.py:128
  723.8 118.8 %collective-permute-start.13 = (f32[4,64,384]{2,1,0:T(8,128)S(1)}, f32[4,64,384]{2,1,0:T(8,128)S(1)}, u32[]{:S(2)}, u32[]{:S(2)}) collective-permute-start(f32[4,64,384]{2,1,0:T(8,128)S(1)} %get-tuple-element.747), channel_id=1, source_target_pairs={{8,0},{16,8},{24,16},{0,24},{9,1},{17,9},{25,17},{1,25},{10,2},{18... | collective-permute-start | bytes 1179656 | tf_op jit(solution)/shard_map/ppermute | solution.py:25
  845.6 5.9 collective-permute-done.12
  863.1 12.5 %collective-permute-done.14 = f32[4,512,64]{1,2,0:T(8,128)S(1)} collective-permute-done((f32[4,512,64]{1,2,0:T(8,128)}, f32[4,512,64]{1,2,0:T(8,128)S(1)}, u32[]{:S(2)}, u32[]{:S(2)}) %collective-permute-start.14) | collective-permute-done | bytes 524320 | tf_op jit(solution)/shard_map/ppermute | solution.py:22
  883.1 77.2 %all-gather.7.cloned.1.call-done = f32[64,256,256]{2,1,0:T(8,128)} async-done(((f32[2,256,256]{2,1,0:T(8,128)}), f32[64,256,256]{2,1,0:T(8,128)}) %all-gather.7.cloned.1.call-update) | async-done | bytes 16777232 | tf_op jit(solution)/shard_map/all_gather | solution.py:142
  960.3 6.9 reduce_sum.19
  (357 shorter events, 343.4 us)
Async XLA Ops:
  7.2 501.2 %all-gather.5.cloned.1.call-start = ((), (), s32[]{:S(2)}) async-start(), calls=%async_computation | async-start | bytes 17301504 | tf_op jit(solution)/shard_map/all_gather | solution.py:142
  8.8 40.3 %copy-start.3 = (f32[2,2,256,256]{2,3,1,0:T(8,128)}, f32[2,2,256,256]{2,3,1,0:T(8,128)S(1)}, u32[]{:S(2)}) copy-start(f32[2,2,256,256]{2,3,1,0:T(8,128)S(1)} %copy.21) | copy-start | bytes 3145732
  10.1 16.9 %collective-permute-start = (f32[4,64,256]{1,2,0:T(8,128)}, f32[4,64,256]{1,2,0:T(8,128)S(1)}, u32[]{:S(2)}, u32[]{:S(2)}) collective-permute-start(f32[4,64,256]{1,2,0:T(8,128)} %get-tuple-element.756), channel_id=1, source_target_pairs={{0,8},{8,16},{16,24},{24,0},{1,9},{9,17},{17,25},{25,1},{2,10},{10... | collective-permute-start | bytes 786440 | tf_op jit(solution)/shard_map/ppermute | solution.py:22
  13.0 24.6 %collective-permute-start.1 = (f32[4,64,256]{1,2,0:T(8,128)}, f32[4,64,256]{1,2,0:T(8,128)S(1)}, u32[]{:S(2)}, u32[]{:S(2)}) collective-permute-start(f32[4,64,256]{1,2,0:T(8,128)} %get-tuple-element.757), channel_id=1, source_target_pairs={{8,0},{16,8},{24,16},{0,24},{9,1},{17,9},{25,17},{1,25},{10,2},{18... | collective-permute-start | bytes 786440 | tf_op jit(solution)/shard_map/ppermute | solution.py:25
  37.9 11.2 %collective-permute-start.2 = (f32[4,384,64]{1,2,0:T(8,128)S(1)}, f32[4,384,64]{1,2,0:T(8,128)S(1)}, u32[]{:S(2)}, u32[]{:S(2)}) collective-permute-start(f32[4,384,64]{1,2,0:T(8,128)S(1)} %get-tuple-element.752), channel_id=1, source_target_pairs={{0,1},{1,2},{2,3},{3,4},{4,5},{5,6},{6,7},{7,0},{8,9},{9,10},{10,1... | collective-permute-start | bytes 1179656 | tf_op jit(solution)/shard_map/ppermute | solution.py:22
  38.0 11.1 %collective-permute-start.3 = (f32[4,384,64]{1,2,0:T(8,128)S(1)}, f32[4,384,64]{1,2,0:T(8,128)S(1)}, u32[]{:S(2)}, u32[]{:S(2)}) collective-permute-start(f32[4,384,64]{1,2,0:T(8,128)S(1)} %get-tuple-element.753), channel_id=1, source_target_pairs={{1,0},{2,1},{3,2},{4,3},{5,4},{6,5},{7,6},{0,7},{9,8},{10,9},{11,1... | collective-permute-start | bytes 1179656 | tf_op jit(solution)/shard_map/ppermute | solution.py:25
  123.5 13.5 %copy-start.8 = (f32[2,256,256]{2,1,0:T(8,128)}, f32[2,256,256]{2,1,0:T(8,128)S(1)}, u32[]{:S(2)}) copy-start(f32[2,256,256]{2,1,0:T(8,128)S(1)} %maximum_add_fusion.9) | copy-start | bytes 1572868 | tf_op jit(solution)/shard_map/while
  240.4 13.5 %copy-start.8 = (f32[2,256,256]{2,1,0:T(8,128)}, f32[2,256,256]{2,1,0:T(8,128)S(1)}, u32[]{:S(2)}) copy-start(f32[2,256,256]{2,1,0:T(8,128)S(1)} %maximum_add_fusion.9) | copy-start | bytes 1572868 | tf_op jit(solution)/shard_map/while
  260.3 700.0 %all-gather.7.cloned.1.call-start = ((), (), s32[]{:S(2)}) async-start(), calls=%async_computation.1 | async-start | bytes 17301504 | tf_op jit(solution)/shard_map/all_gather | solution.py:142
  261.5 125.5 %collective-permute-start.4 = (f32[4,64,384]{2,1,0:T(8,128)S(1)}, f32[4,64,384]{2,1,0:T(8,128)}, u32[]{:S(2)}, u32[]{:S(2)}) collective-permute-start(f32[4,64,384]{2,1,0:T(8,128)S(1)} %get-tuple-element.748), channel_id=1, source_target_pairs={{0,8},{8,16},{16,24},{24,0},{1,9},{9,17},{17,25},{25,1},{2,10},{10... | collective-permute-start | bytes 1179656 | tf_op jit(solution)/shard_map/ppermute | solution.py:22
  261.6 129.7 %collective-permute-start.5 = (f32[4,64,384]{2,1,0:T(8,128)S(1)}, f32[4,64,384]{2,1,0:T(8,128)S(1)}, u32[]{:S(2)}, u32[]{:S(2)}) collective-permute-start(f32[4,64,384]{2,1,0:T(8,128)S(1)} %get-tuple-element.749), channel_id=1, source_target_pairs={{8,0},{16,8},{24,16},{0,24},{9,1},{17,9},{25,17},{1,25},{10,2},{18... | collective-permute-start | bytes 1179656 | tf_op jit(solution)/shard_map/ppermute | solution.py:25
  394.1 20.2 %collective-permute-start.6 = (f32[4,512,64]{1,2,0:T(8,128)}, f32[4,512,64]{1,2,0:T(8,128)}, u32[]{:S(2)}, u32[]{:S(2)}) collective-permute-start(f32[4,512,64]{1,2,0:T(8,128)} %get-tuple-element.740), channel_id=1, source_target_pairs={{0,1},{1,2},{2,3},{3,4},{4,5},{5,6},{6,7},{7,0},{8,9},{9,10},{10,1... | collective-permute-start | bytes 1572872 | tf_op jit(solution)/shard_map/ppermute | solution.py:22
  399.9 14.6 %collective-permute-start.7 = (f32[4,512,64]{1,2,0:T(8,128)}, f32[4,512,64]{1,2,0:T(8,128)}, u32[]{:S(2)}, u32[]{:S(2)}) collective-permute-start(f32[4,512,64]{1,2,0:T(8,128)} %get-tuple-element.741), channel_id=1, source_target_pairs={{1,0},{2,1},{3,2},{4,3},{5,4},{6,5},{7,6},{0,7},{9,8},{10,9},{11,1... | collective-permute-start | bytes 1572872 | tf_op jit(solution)/shard_map/ppermute | solution.py:25
  401.2 16.2 %copy-start.2 = (f32[4,384,384]{1,2,0:T(8,128)S(1)}, f32[4,384,384]{1,2,0:T(8,128)}, u32[]{:S(2)}) copy-start(f32[4,384,384]{1,2,0:T(8,128)} %copy.25) | copy-start | bytes 7077892
  422.0 76.8 %copy-start.5 = (f32[4,256,256]{1,2,0:T(8,128)}, f32[4,256,256]{1,2,0:T(8,128)S(1)}, u32[]{:S(2)}) copy-start(f32[4,256,256]{1,2,0:T(8,128)S(1)} %fusion.249) | copy-start | bytes 3145732
  422.2 20.7 %collective-permute-start.8 = (f32[4,64,256]{1,2,0:T(8,128)S(1)}, f32[4,64,256]{1,2,0:T(8,128)S(1)}, u32[]{:S(2)}, u32[]{:S(2)}) collective-permute-start(f32[4,64,256]{1,2,0:T(8,128)S(1)} %get-tuple-element.754), channel_id=1, source_target_pairs={{0,8},{8,16},{16,24},{24,0},{1,9},{9,17},{17,25},{25,1},{2,10},{10... | collective-permute-start | bytes 786440 | tf_op jit(solution)/shard_map/ppermute | solution.py:22
  435.6 25.9 %collective-permute-start.9 = (f32[4,64,256]{1,2,0:T(8,128)S(1)}, f32[4,64,256]{1,2,0:T(8,128)S(1)}, u32[]{:S(2)}, u32[]{:S(2)}) collective-permute-start(f32[4,64,256]{1,2,0:T(8,128)S(1)} %get-tuple-element.755), channel_id=1, source_target_pairs={{8,0},{16,8},{24,16},{0,24},{9,1},{17,9},{25,17},{1,25},{10,2},{18... | collective-permute-start | bytes 786440 | tf_op jit(solution)/shard_map/ppermute | solution.py:25
  463.6 18.1 %collective-permute-start.10 = (f32[4,384,64]{1,2,0:T(8,128)}, f32[4,384,64]{1,2,0:T(8,128)S(1)}, u32[]{:S(2)}, u32[]{:S(2)}) collective-permute-start(f32[4,384,64]{1,2,0:T(8,128)} %get-tuple-element.750), channel_id=1, source_target_pairs={{0,1},{1,2},{2,3},{3,4},{4,5},{5,6},{6,7},{7,0},{8,9},{9,10},{10,1... | collective-permute-start | bytes 1179656 | tf_op jit(solution)/shard_map/ppermute | solution.py:22
  480.1 15.5 %collective-permute-start.11 = (f32[4,384,64]{1,2,0:T(8,128)}, f32[4,384,64]{1,2,0:T(8,128)}, u32[]{:S(2)}, u32[]{:S(2)}) collective-permute-start(f32[4,384,64]{1,2,0:T(8,128)} %get-tuple-element.751), channel_id=1, source_target_pairs={{1,0},{2,1},{3,2},{4,3},{5,4},{6,5},{7,6},{0,7},{9,8},{10,9},{11,1... | collective-permute-start | bytes 1179656 | tf_op jit(solution)/shard_map/ppermute | solution.py:25
  723.7 127.8 %collective-permute-start.12 = (f32[4,64,384]{2,1,0:T(8,128)S(1)}, f32[4,64,384]{2,1,0:T(8,128)S(1)}, u32[]{:S(2)}, u32[]{:S(2)}) collective-permute-start(f32[4,64,384]{2,1,0:T(8,128)S(1)} %get-tuple-element.746), channel_id=1, source_target_pairs={{0,8},{8,16},{16,24},{24,0},{1,9},{9,17},{17,25},{25,1},{2,10},{10... | collective-permute-start | bytes 1179656 | tf_op jit(solution)/shard_map/ppermute | solution.py:22
  723.8 131.7 %collective-permute-start.13 = (f32[4,64,384]{2,1,0:T(8,128)S(1)}, f32[4,64,384]{2,1,0:T(8,128)S(1)}, u32[]{:S(2)}, u32[]{:S(2)}) collective-permute-start(f32[4,64,384]{2,1,0:T(8,128)S(1)} %get-tuple-element.747), channel_id=1, source_target_pairs={{8,0},{16,8},{24,16},{0,24},{9,1},{17,9},{25,17},{1,25},{10,2},{18... | collective-permute-start | bytes 1179656 | tf_op jit(solution)/shard_map/ppermute | solution.py:25
  858.3 17.3 %collective-permute-start.14 = (f32[4,512,64]{1,2,0:T(8,128)}, f32[4,512,64]{1,2,0:T(8,128)S(1)}, u32[]{:S(2)}, u32[]{:S(2)}) collective-permute-start(f32[4,512,64]{1,2,0:T(8,128)} %get-tuple-element.738), channel_id=1, source_target_pairs={{0,1},{1,2},{2,3},{3,4},{4,5},{5,6},{6,7},{7,0},{8,9},{9,10},{10,1... | collective-permute-start | bytes 1572872 | tf_op jit(solution)/shard_map/ppermute | solution.py:22
  861.2 14.3 %collective-permute-start.15 = (f32[4,512,64]{1,2,0:T(8,128)}, f32[4,512,64]{1,2,0:T(8,128)S(1)}, u32[]{:S(2)}, u32[]{:S(2)}) collective-permute-start(f32[4,512,64]{1,2,0:T(8,128)} %get-tuple-element.739), channel_id=1, source_target_pairs={{1,0},{2,1},{3,2},{4,3},{5,4},{6,5},{7,6},{0,7},{9,8},{10,9},{11,1... | collective-permute-start | bytes 1572872 | tf_op jit(solution)/shard_map/ppermute | solution.py:25
  863.1 15.3 %copy-start.1 = (f32[4,384,384]{1,2,0:T(8,128)S(1)}, f32[4,384,384]{1,2,0:T(8,128)}, u32[]{:S(2)}) copy-start(f32[4,384,384]{1,2,0:T(8,128)} %copy.30) | copy-start | bytes 7077892
  (16 other events, 63.4 us)
Sparse Core Ops, SparseCore 0:
  260.4 247.9 all-gather.4
  722.7 237.5 all-gather.6
